TPU v7x, 32 devices: a whole 2x2x4 slice. The times are simulated.
32 devices in a mesh: batch: 2 (over core), neuron: 16 (over z, y, x).
Axes of the slice: x: 2, y: 2, z: 4, core: 2. Of those that a mesh axis runs over, the one named last changes fastest.
Arguments:
- images: bfloat16 [32, 65536], P('batch', 'neuron'), parts along dimension 0, may hold values from 0 to 32
- tile_weights: bfloat16 [2, 2048, 128, 128], P(None, 'neuron'), may hold values from -0.375 to 0.375
- tile_blocks: int32 [2, 2048, 2], P(None, 'neuron'), may hold values from 0 to 511, as said below
- tile_count: int32 [2, 16], P(None, 'neuron'), may hold values from 96 to 128, as said below
- bias: float32 [2, 65536], P(None, 'neuron'), may hold values from -48 to 48
Outputs:
- activity: bfloat16 [32, 65536], P('batch', 'neuron'), parts along dimension 0
There are 2 independent parts, one for each index of `batch`. A program takes and returns all parts, laid end to end along the dimension named above; an argument that names none is the same for every part. Nothing has to cross between parts.
Inputs may be any that keep to these rules, and one draw needn't show every extreme that they name: Slots 0 to tile_count[l, d] - 1 of device d are live in layer l; in every layer one device has all 128 live. `tile_blocks`: entry [l, d * 128 + s, :] is the row block and column block of slot s of device d. Within one device and layer the column blocks are all different, and at most 8 of them lie among the 32 column blocks of any one neuron device; in every layer the column blocks of some neuron device get exactly 8 live slots from every device.
All inputs are finite; a program needn't handle non-finite values.
Results may differ from a plain program's by a relative error of at most 0.0033.
Values may be sent and summed in bfloat16 or wider, within the bound.
A program may use at most 64 MiB of HBM per device.

v0:
```python
import jax
import jax.numpy as jnp
from jax import lax
from jax.sharding import PartitionSpec as P

CEILING = 32.0


def local(images, tile_weights, tile_blocks, tile_count, bias):
    devices = lax.axis_size("neuron")
    layer_total = tile_weights.shape[0]
    slot_total = tile_weights.shape[1]
    block_width = tile_weights.shape[2]
    image_rows, local_width = images.shape
    own_blocks = local_width // block_width
    all_blocks = own_blocks * devices
    capacity = max(2, slot_total // devices)
    slot_ids = jnp.arange(slot_total, dtype=jnp.int32)
    activity = images
    for layer_index in range(layer_total):
        whole_acts = lax.all_gather(activity, "neuron", axis=1, tiled=True)
        block_view = whole_acts.reshape(image_rows, all_blocks, block_width)
        row_ids = tile_blocks[layer_index, :, 0]
        col_ids = tile_blocks[layer_index, :, 1]
        usable = slot_ids < tile_count[layer_index, 0]
        picked = jnp.take(block_view, row_ids, axis=1)
        products = jnp.einsum(
            "bsk,skn->sbn", picked, tile_weights[layer_index], preferred_element_type=jnp.float32
        )
        products = jnp.where(usable[:, None, None], products, 0.0)
        owners = col_ids // own_blocks
        local_block = (col_ids % own_blocks).astype(jnp.float32)
        same_owner = (
            (owners[:, None] == owners[None, :])
            & usable[None, :]
            & (slot_ids[None, :] < slot_ids[:, None])
        )
        slot_rank = jnp.sum(same_owner.astype(jnp.int32), axis=1)
        targets = jnp.where(usable, owners * capacity + slot_rank, devices * capacity)
        outgoing = (
            jnp.zeros((devices * capacity, image_rows, block_width), jnp.float32)
            .at[targets]
            .set(products, mode="drop")
        )
        labels = (
            jnp.full((devices * capacity,), -1.0, jnp.float32)
            .at[targets]
            .set(local_block, mode="drop")
        )
        incoming, arrived_ids = (
            lax.all_to_all(outgoing, "neuron", split_axis=0, concat_axis=0, tiled=True),
            lax.all_to_all(labels, "neuron", split_axis=0, concat_axis=0, tiled=True),
        )
        selector = (
            arrived_ids[None, :] == jnp.arange(own_blocks, dtype=jnp.float32)[:, None]
        ).astype(jnp.float32)
        summed = jnp.einsum("or,rbn->obn", selector, incoming, precision=lax.Precision.HIGHEST)
        summed = jnp.transpose(summed, (1, 0, 2)).reshape(image_rows, local_width)
        activity = jnp.clip(summed + bias[layer_index][None, :], 0.0, CEILING).astype(jnp.bfloat16)
    return activity


def solution(mesh):
    in_specs = (
        P("batch", "neuron"),
        P(None, "neuron", None, None),
        P(None, "neuron", None),
        P(None, "neuron"),
        P(None, "neuron"),
    )
    out_specs = P("batch", "neuron")
    return jax.shard_map(local, mesh=mesh, in_specs=in_specs, out_specs=out_specs, check_vma=False)
```

profile of v0, /device:TPU:0, one launch (start us, length us, event | category | flops | bytes accessed | tf_op | source)
XLA Modules:
  0.0 240.6 jit_solution(3494090513267543889)
XLA Ops:
  6.5 0.0 all-gather.3.cloned.1.call-start
  6.5 0.7 all-gather.3.cloned.1.call-update
  7.3 1.3 fusion.47
  8.5 0.6 iota_compare_fusion.3
  9.2 0.6 iota_compare_fusion.4
  9.8 0.7 fusion.37
  10.4 0.7 fusion.36
  11.2 0.7 and_select_fusion.4
  11.8 0.2 convert_reduce_fusion
  12.0 1.9 fusion.39
  13.9 1.0 scatter_custom_fusion.1
  14.9 0.7 all_to_all.20
  15.6 8.3 %all-to-all-start.1 = ((f32[16,8,1]{1,2,0:T(1,128)}), f32[16,8,1]{1,2,0:T(1,128)S(1)}, u32[]{:S(2)}, u32[]{:S(2)}) async-start(f32[16,8,1]{1,2,0:T(1,128)} %bitcast.13), calls=%async_computation.1 | async-start | bytes 16384 | tf_op jit(solution)/shard_map/all_to_all | solution.py:52
  24.0 0.7 compare_and_fusion
  24.7 48.5 %all-gather.3.cloned.1.call-done = bf16[16,65536]{1,0:T(8,128)(2,1)} async-done(((bf16[16,4096]{1,0:T(8,128)(2,1)}), bf16[16,65536]{1,0:T(8,128)(2,1)}) %all-gather.3.cloned.1.call-update) | async-done | bytes 2097168 | tf_op jit(solution)/shard_map/all_gather | solution.py:21
  73.1 2.0 copy_bitcast_fusion.1
  75.1 0.7 gather_fusion
  75.8 3.2 %fusion.6 = f32[128,16,128]{2,1,0:T(8,128)S(1)} fusion(bf16[2,128,128,128]{3,2,1,0:T(8,128)(2,1)} %param.8, bf16[128,16,128]{2,1,0:T(8,128)(2,1)S(1)} %gather_fusion, pred[128]{0:T(512)(128)(4,1)S(1)} %get-tuple-element.16, pred[128]{0:T(512)(128)(4,1)S(1)} %iota_compare_fusion.3), kind=kOutput, calls=%fused_computation.14 | convolution fusion | flops 67633152 | bytes 5767424 | tf_op jit(solution)/shard_map/bsk,skn->sbn/dot_general | solution.py:27
  79.0 1.0 broadcast.299.clone
  80.0 0.0 copy-start
  80.0 13.5 %scatter_fusion = f32[128,16,128]{2,1,0:T(8,128)} fusion(f32[128,16,128]{2,1,0:T(8,128)} %broadcast.299.clone, s32[128]{0:T(128)S(1)} %get-tuple-element.18, f32[128,16,128]{2,1,0:T(8,128)S(1)} %fusion.6), kind=kCustom, calls=%fused_computation.4 | custom fusion | bytes 3146240 | tf_op jit(solution)/shard_map/scatter | solution.py:43
  93.6 0.0 all-to-all-done.1
  93.6 4.5 %all-to-all-start.2 = ((f32[128,16,128]{2,1,0:T(8,128)}), f32[128,16,128]{2,1,0:T(8,128)S(1)}, u32[]{:S(2)}, u32[]{:S(2)}) async-start(f32[128,16,128]{2,1,0:T(8,128)} %scatter_fusion), calls=%async_computation.2 | async-start | bytes 2097152 | tf_op jit(solution)/shard_map/all_to_all | solution.py:51
  98.1 0.0 all-gather.5.cloned.1.call-start
  98.1 0.0 copy-done
  98.2 0.6 broadcast.370
  98.7 0.6 reduce.6
  99.4 0.1 eq.69
  99.5 22.0 %all-to-all-done.2 = f32[128,16,128]{2,1,0:T(8,128)S(1)} async-done(((f32[128,16,128]{2,1,0:T(8,128)}), f32[128,16,128]{2,1,0:T(8,128)S(1)}, u32[]{:S(2)}, u32[]{:S(2)}) %all-to-all-start.2) | async-done | bytes 1048608 | tf_op jit(solution)/shard_map/all_to_all | solution.py:51
  121.5 0.7 fusion.14
  122.2 0.8 fusion.25
  123.0 0.0 all-gather.5.cloned.1.call-update
  123.1 1.0 scatter_custom_fusion
  124.1 0.7 all_to_all.18
  124.7 5.9 %all-to-all-start = ((f32[16,8,1]{1,2,0:T(1,128)}), f32[16,8,1]{1,2,0:T(1,128)S(1)}, u32[]{:S(2)}, u32[]{:S(2)}) async-start(f32[16,8,1]{1,2,0:T(1,128)} %bitcast.5), calls=%async_computation | async-start | bytes 16384 | tf_op jit(solution)/shard_map/all_to_all | solution.py:52
  130.6 53.1 %all-gather.5.cloned.1.call-done = bf16[16,65536]{1,0:T(8,128)(2,1)} async-done(((bf16[16,4096]{1,0:T(8,128)(2,1)}), bf16[16,65536]{1,0:T(8,128)(2,1)}) %all-gather.5.cloned.1.call-update) | async-done | bytes 2097168 | tf_op jit(solution)/shard_map/all_gather | solution.py:21
  183.8 2.0 copy_bitcast_fusion
  185.7 0.7 gather_fusion.1
  186.4 3.2 %fusion.9 = f32[128,16,128]{2,1,0:T(8,128)S(1)} fusion(bf16[2,128,128,128]{3,2,1,0:T(8,128)(2,1)} %param.8, bf16[128,16,128]{2,1,0:T(8,128)(2,1)S(1)} %gather_fusion.1, pred[128]{0:T(512)(128)(4,1)S(1)} %get-tuple-element.8, pred[128]{0:T(512)(128)(4,1)S(1)} %iota_compare_fusion.4), kind=kOutput, calls=%fused_computation.15 | convolution fusion | flops 67633152 | bytes 5767424 | tf_op jit(solution)/shard_map/bsk,skn->sbn/dot_general | solution.py:27
  189.6 1.0 broadcast.299
  190.6 13.8 %scatter_fusion.1 = f32[128,16,128]{2,1,0:T(8,128)} fusion(f32[128,16,128]{2,1,0:T(8,128)} %broadcast.299, s32[128]{0:T(128)S(1)} %get-tuple-element.19, f32[128,16,128]{2,1,0:T(8,128)S(1)} %fusion.9), kind=kCustom, calls=%fused_computation.5 | custom fusion | bytes 3146240 | tf_op jit(solution)/shard_map/scatter | solution.py:43
  204.5 0.0 all-to-all-done
  204.5 4.2 %all-to-all-start.3 = ((f32[128,16,128]{2,1,0:T(8,128)}), f32[128,16,128]{2,1,0:T(8,128)S(1)}, u32[]{:S(2)}, u32[]{:S(2)}) async-start(f32[128,16,128]{2,1,0:T(8,128)} %scatter_fusion.1), calls=%async_computation.3 | async-start | bytes 2097152 | tf_op jit(solution)/shard_map/all_to_all | solution.py:51
  208.6 0.6 reduce.7
  209.3 0.1 eq.62
  209.4 22.8 %all-to-all-done.3 = f32[128,16,128]{2,1,0:T(8,128)S(1)} async-done(((f32[128,16,128]{2,1,0:T(8,128)}), f32[128,16,128]{2,1,0:T(8,128)S(1)}, u32[]{:S(2)}, u32[]{:S(2)}) %all-to-all-start.3) | async-done | bytes 1048608 | tf_op jit(solution)/shard_map/all_to_all | solution.py:51
  232.2 0.7 fusion.12
  232.9 0.8 fusion.23
  (3 shorter events, 0.0 us)
Async XLA Ops:
  6.5 66.6 %all-gather.3.cloned.1.call-start = ((), (), s32[]{:S(2)}) async-start(), calls=%async_computation.4 | async-start | bytes 2228224 | tf_op jit(solution)/shard_map/all_gather | solution.py:21
  15.6 78.0 %all-to-all-start.1 = ((f32[16,8,1]{1,2,0:T(1,128)}), f32[16,8,1]{1,2,0:T(1,128)S(1)}, u32[]{:S(2)}, u32[]{:S(2)}) async-start(f32[16,8,1]{1,2,0:T(1,128)} %bitcast.13), calls=%async_computation.1 | async-start | bytes 16384 | tf_op jit(solution)/shard_map/all_to_all | solution.py:52
  80.0 18.1 %copy-start = (f32[2,4096]{1,0:T(2,128)S(1)}, f32[2,4096]{1,0:T(2,128)}, u32[]{:S(2)}) copy-start(f32[2,4096]{1,0:T(2,128)} %param.11) | copy-start | bytes 98308
  93.6 27.9 %all-to-all-start.2 = ((f32[128,16,128]{2,1,0:T(8,128)}), f32[128,16,128]{2,1,0:T(8,128)S(1)}, u32[]{:S(2)}, u32[]{:S(2)}) async-start(f32[128,16,128]{2,1,0:T(8,128)} %scatter_fusion), calls=%async_computation.2 | async-start | bytes 2097152 | tf_op jit(solution)/shard_map/all_to_all | solution.py:51
  98.1 85.7 %all-gather.5.cloned.1.call-start = ((), (), s32[]{:S(2)}) async-start(), calls=%async_computation.5 | async-start | bytes 2228224 | tf_op jit(solution)/shard_map/all_gather | solution.py:21
  124.7 79.7 %all-to-all-start = ((f32[16,8,1]{1,2,0:T(1,128)}), f32[16,8,1]{1,2,0:T(1,128)S(1)}, u32[]{:S(2)}, u32[]{:S(2)}) async-start(f32[16,8,1]{1,2,0:T(1,128)} %bitcast.5), calls=%async_computation | async-start | bytes 16384 | tf_op jit(solution)/shard_map/all_to_all | solution.py:52
  204.5 27.7 %all-to-all-start.3 = ((f32[128,16,128]{2,1,0:T(8,128)}), f32[128,16,128]{2,1,0:T(8,128)S(1)}, u32[]{:S(2)}, u32[]{:S(2)}) async-start(f32[128,16,128]{2,1,0:T(8,128)} %scatter_fusion.1), calls=%async_computation.3 | async-start | bytes 2097152 | tf_op jit(solution)/shard_map/all_to_all | solution.py:51
Sparse Core Ops, SparseCore 0:
  10.1 63.0 all-gather.2
  123.2 60.5 all-gather.4
where the time goes:
time: 242 us; the launch traced here: 241 us
  waiting for transfers between devices  147 us (61%)
  local copies, waits for them, and re-layouts  40.1 us (17%)
  starting transfers between devices  22.9 us (9%)
  between operations  13.6 us (6%)
  other arithmetic  9.02 us (4%)
  matrix products  7.83 us (3%)
    all_gather x2, waiting for transfers between devices, local(): whole_acts = lax.all_gather(activity, 'neuron', axis=1, tiled=True)  102 us
    all_to_all x2, waiting for transfers between devices, local(): lax.all_to_all(outgoing, 'neuron', split_axis=0, concat_axis=0, tiled=True)  44.8 us
    scatter x2, local copies, waits for them, and re-layouts, local(): outgoing = jnp.zeros((devices * capacity, image_rows, block_width), jnp.f...  27.4 us
    all_to_all x2, starting transfers between devices, local(): lax.all_to_all(labels, 'neuron', split_axis=0, concat_axis=0, tiled=True)  14.2 us
    all_to_all x2, starting transfers between devices, local(): lax.all_to_all(outgoing, 'neuron', split_axis=0, concat_axis=0, tiled=True)  8.66 us
    dot_general x2, matrix products, local(): jnp.einsum('bsk,skn->sbn', picked, tile_weights[layer_index], preferred_e...  6.35 us
  transfers between devices with their start and end apart: 6, of which 4 were waited for; matrix products, arithmetic and copies ran while one was open for 22% of the time, Pallas kernels for 0%

commit v1 on v0

v1 whole, which is shorter than its diff:
```python
import functools

import jax
import jax.numpy as jnp
from jax import lax
from jax.experimental import pallas as pl
from jax.experimental.pallas import tpu as pltpu
from jax.sharding import PartitionSpec as P

CEILING = 32.0
SENT = (jnp.float32, jnp.bfloat16)


def sides(devices):
    side = 1
    while 2 * side**3 < devices:
        side += 1
    if 2 * side**3 == devices:
        return 2 * side, side, side
    return devices, 1, 1


def paired(here, step, extent):
    if extent & (extent - 1):
        return lax.rem(here + step, extent)
    there, bit = 0, 1
    while bit < extent:
        there = there + (((here // bit) % 2 + (step // bit) % 2) % 2) * bit
        bit *= 2
    return there


def kernel(
    layers, devices, own, capacity,
    table, place, images, weights_hbm, bias, out,
    acts, weights, outgoing, incoming, place_in, place_smem,
    weight_sem, place_send, place_recv, smem_sem,
    z_send, z_recv, half_send, half_recv, pass_send, part_send, part_recv,
):
    me = lax.axis_index("neuron")
    zs, ys, xs = sides(devices)
    z, y, x = me // (ys * xs), (me // xs) % ys, me % xs
    slots = devices * capacity
    half = own // 2

    def index(zz, yy, xx):
        return (zz * ys + yy) * xs + xx

    def remote(src, dst, send, recv, target):
        copy = pltpu.make_async_remote_copy(
            src_ref=src, dst_ref=dst, send_sem=send, recv_sem=recv,
            device_id={"neuron": target}, device_id_type=pl.DeviceIdType.MESH,
        )
        copy.start()
        return copy

    def partner(t):
        q, i = t // (ys * xs), t % (ys * xs)
        return index(
            paired(z, zs - 1 - q, zs),
            paired(y, ys - 1 - i // xs, ys),
            paired(x, xs - 1 - i % xs, xs),
        )

    loads = []
    for layer in range(layers):
        load = pltpu.make_async_copy(weights_hbm.at[layer], weights[layer], weight_sem.at[layer])
        load.start()
        loads.append(load)

    barrier = pltpu.get_barrier_semaphore()

    def greet(t, carry):
        pl.semaphore_signal(
            barrier, inc=1, device_id={"neuron": partner(t)}, device_id_type=pl.DeviceIdType.MESH
        )
        return carry

    lax.fori_loop(0, devices - 1, greet, 0)
    for c in range(own):
        acts[0][me * own + c] = images[:, c * 128 : (c + 1) * 128]
    for layer in range(layers):
        incoming[layer][slots] = jnp.zeros(incoming[layer].shape[1:], incoming[layer].dtype)
    place_in[me] = place[me]
    pl.semaphore_wait(barrier, devices - 1)

    def place_copy(t):
        target = partner(t)
        return pltpu.make_async_remote_copy(
            src_ref=place.at[target], dst_ref=place_in.at[me],
            send_sem=place_send.at[t], recv_sem=place_recv.at[me],
            device_id={"neuron": target}, device_id_type=pl.DeviceIdType.MESH,
        )

    for layer in range(layers):
        pending = []

        def piece(owner, part):
            return acts[layer].at[pl.ds(owner * own + part * half, half)]

        def arrived(ref, sem):
            pltpu.make_async_copy(ref, ref, sem).wait()

        mine = acts[layer].at[pl.ds(me * own, own)]
        for m in range(1, zs):
            pending.append(
                remote(mine, mine, z_send.at[layer, m], z_recv.at[layer, z],
                       index(paired(z, m, zs), y, x))
            )

        def spread(m):
            zz = paired(z, m, zs)
            owner = index(zz, y, x)
            if m:
                shard = acts[layer].at[pl.ds(owner * own, own)]
                arrived(shard, z_recv.at[layer, zz])
            slot = 0
            for first in (True, False):
                for n in range(1, ys):
                    part = 0 if first else 1
                    pending.append(
                        remote(piece(owner, part), piece(owner, part),
                               half_send.at[layer, m, slot], half_recv.at[layer, owner, part],
                               index(z, paired(y, n, ys), x))
                    )
                    slot += 1
                for n in range(1, xs):
                    part = 1 if first else 0
                    pending.append(
                        remote(piece(owner, part), piece(owner, part),
                               half_send.at[layer, m, slot], half_recv.at[layer, owner, part],
                               index(z, y, paired(x, n, xs)))
                    )
                    slot += 1

        def relay(m):
            zz = paired(z, m, zs)
            slot = 0
            for n in range(1, ys):
                owner = index(zz, paired(y, n, ys), x)
                arrived(piece(owner, 0), half_recv.at[layer, owner, 0])
                for k in range(1, xs):
                    pending.append(
                        remote(piece(owner, 0), piece(owner, 0),
                               pass_send.at[layer, m, slot], half_recv.at[layer, owner, 0],
                               index(z, y, paired(x, k, xs)))
                    )
                    slot += 1
            for n in range(1, xs):
                owner = index(zz, y, paired(x, n, xs))
                arrived(piece(owner, 1), half_recv.at[layer, owner, 1])
                for k in range(1, ys):
                    pending.append(
                        remote(piece(owner, 1), piece(owner, 1),
                               pass_send.at[layer, m, slot], half_recv.at[layer, owner, 1],
                               index(z, paired(y, k, ys), x))
                    )
                    slot += 1

        spread(0)
        if layer == 0:
            def send_place(t, carry):
                place_copy(t).start()
                return carry

            lax.fori_loop(0, devices - 1, send_place, 0)
        for m in range(1, zs):
            spread(m)
            relay(m - 1)
        relay(zs - 1)

        for m in range(zs):
            zz = paired(z, m, zs)
            for n in range(1, ys):
                owner = index(zz, paired(y, n, ys), x)
                arrived(piece(owner, 1), half_recv.at[layer, owner, 1])
            for n in range(1, xs):
                owner = index(zz, y, paired(x, n, xs))
                arrived(piece(owner, 0), half_recv.at[layer, owner, 0])
            for n in range(1, ys):
                for k in range(1, xs):
                    owner = index(zz, paired(y, n, ys), paired(x, k, xs))
                    for part in range(2):
                        arrived(piece(owner, part), half_recv.at[layer, owner, part])
        loads[layer].wait()

        out_buf, in_buf = outgoing[layer], incoming[layer]

        def product(target, k):
            at = layer * 2 * slots + target * capacity + k
            block = acts[layer][table[at]]
            tile = weights[layer][table[at + slots]]
            return jnp.dot(block, tile, preferred_element_type=jnp.float32).astype(out_buf.dtype)

        def part_copy(t):
            target = partner(t)
            return pltpu.make_async_remote_copy(
                src_ref=out_buf.at[pl.ds(target * capacity, capacity)],
                dst_ref=in_buf.at[pl.ds(me * capacity, capacity)],
                send_sem=part_send.at[layer, t], recv_sem=part_recv.at[layer, me],
                device_id={"neuron": target}, device_id_type=pl.DeviceIdType.MESH,
            )

        def step(t, carry):
            target = partner(t)
            for k in range(capacity):
                out_buf[target * capacity + k] = product(target, k)
            part_copy(t).start()
            return carry

        lax.fori_loop(0, devices - 1, step, 0)
        for k in range(capacity):
            in_buf[me * capacity + k] = product(me, k)

        if layer == 0:
            def take_place(t, carry):
                ref = place_in.at[partner(t)]
                pltpu.make_async_copy(ref, ref, place_recv.at[partner(t)]).wait()
                return carry

            lax.fori_loop(0, devices - 1, take_place, 0)
            to_smem = pltpu.make_async_copy(place_in, place_smem, smem_sem)
            to_smem.start()
            to_smem.wait()

        def take_part(t, carry):
            source = partner(t)
            ref = in_buf.at[pl.ds(source * capacity, capacity)]
            pltpu.make_async_copy(ref, ref, part_recv.at[layer, source]).wait()
            return carry

        lax.fori_loop(0, devices - 1, take_part, 0)

        def combine(c, carry):
            total = jnp.broadcast_to(
                bias[pl.ds(layer, 1), pl.ds(pl.multiple_of(c * 128, 128), 128)], in_buf.shape[1:]
            )
            for source in range(devices):
                at = place_smem[source, 0, layer * own + c]
                total = total + in_buf[at].astype(jnp.float32)
            value = jnp.minimum(jnp.maximum(total, 0.0), CEILING).astype(jnp.bfloat16)
            if layer + 1 < layers:
                acts[layer + 1][me * own + c] = value
            else:
                out[:, pl.ds(pl.multiple_of(c * 128, 128), 128)] = value
            return carry

        lax.fori_loop(0, own, combine, 0)

        for copy in pending:
            copy.wait_send()

        def drain(t, carry):
            part_copy(t).wait_send()
            if layer == 0:
                place_copy(t).wait_send()
            return carry

        lax.fori_loop(0, devices - 1, drain, 0)


def tables(tile_blocks, tile_count, devices, own, capacity):
    layers, slot_total, _ = tile_blocks.shape
    me = lax.axis_index("neuron")
    slots = devices * capacity
    row_ids, col_ids = tile_blocks[:, :, 0], tile_blocks[:, :, 1]
    slot_ids = jnp.arange(slot_total, dtype=jnp.int32)
    usable = slot_ids[None, :] < tile_count
    owners = jnp.where(usable, col_ids // own, -1)
    earlier = (owners[:, :, None] == owners[:, None, :]) & (slot_ids[None, :] < slot_ids[:, None])
    rank = jnp.sum(earlier.astype(jnp.int32), axis=2)
    dest = jnp.where(usable, owners * capacity + rank, -1)
    hit = dest[:, None, :] == jnp.arange(slots, dtype=jnp.int32)[:, None]
    rows = jnp.sum(jnp.where(hit, row_ids[:, None, :], 0), axis=2)
    tiles = jnp.sum(jnp.where(hit, slot_ids, 0), axis=2)
    table = jnp.stack([rows, tiles], axis=1).reshape(-1)
    live_cols = jnp.where(usable, col_ids, -1)
    match = live_cols[:, None, :] == jnp.arange(devices * own, dtype=jnp.int32)[:, None]
    place = slots + jnp.sum(jnp.where(match, me * capacity + rank[:, None, :] - slots, 0), axis=2)
    place = jnp.transpose(place.reshape(layers, devices, own), (1, 0, 2)).reshape(devices, 1, layers * own)
    width = -(-layers * own // 128) * 128
    return table, jnp.pad(place, ((0, 0), (0, 0), (0, width - layers * own)))


def local(images, tile_weights, tile_blocks, tile_count, bias):
    devices = lax.axis_size("neuron")
    layers, slot_total, block, _ = tile_weights.shape
    image_rows, local_width = images.shape
    own = local_width // block
    capacity = max(2, slot_total // devices)
    slots = devices * capacity
    zs, ys, xs = sides(devices)
    table, place = tables(tile_blocks, tile_count, devices, own, capacity)
    width = place.shape[2]
    sent = [SENT[min(layer, len(SENT) - 1)] for layer in range(layers)]
    fan = 2 * (ys + xs)
    vmem = pl.BlockSpec(memory_space=pltpu.VMEM)
    return pl.pallas_call(
        functools.partial(kernel, layers, devices, own, capacity),
        out_shape=jax.ShapeDtypeStruct((image_rows, local_width), jnp.bfloat16),
        in_specs=[
            pl.BlockSpec(memory_space=pltpu.SMEM), vmem, vmem,
            pl.BlockSpec(memory_space=pl.ANY), vmem,
        ],
        out_specs=vmem,
        scratch_shapes=[
            [pltpu.VMEM((devices * own, image_rows, block), jnp.bfloat16)] * layers,
            [pltpu.VMEM((slot_total, block, block), jnp.bfloat16)] * layers,
            [pltpu.VMEM((slots, image_rows, block), kind) for kind in sent],
            [pltpu.VMEM((slots + 1, image_rows, block), kind) for kind in sent],
            pltpu.VMEM((devices, 1, width), jnp.int32),
            pltpu.SMEM((devices, 1, width), jnp.int32),
            pltpu.SemaphoreType.DMA((layers,)),
            pltpu.SemaphoreType.DMA((devices,)),
            pltpu.SemaphoreType.DMA((devices,)),
            pltpu.SemaphoreType.DMA,
            pltpu.SemaphoreType.DMA((layers, zs)),
            pltpu.SemaphoreType.DMA((layers, zs)),
            pltpu.SemaphoreType.DMA((layers, zs, fan)),
            pltpu.SemaphoreType.DMA((layers, devices, 2)),
            pltpu.SemaphoreType.DMA((layers, zs, 2 * ys * xs)),
            pltpu.SemaphoreType.DMA((layers, devices)),
            pltpu.SemaphoreType.DMA((layers, devices)),
        ],
        compiler_params=pltpu.CompilerParams(
            collective_id=0, has_side_effects=True, vmem_limit_bytes=48 * 1024 * 1024
        ),
    )(table, place, images, tile_weights, bias)


def solution(mesh):
    in_specs = (
        P("batch", "neuron"),
        P(None, "neuron", None, None),
        P(None, "neuron", None),
        P(None, "neuron"),
        P(None, "neuron"),
    )
    out_specs = P("batch", "neuron")
    return jax.shard_map(local, mesh=mesh, in_specs=in_specs, out_specs=out_specs, check_vma=False)
```

time: 242 us -> 93.1 us (0.38)
  waiting for transfers between devices: 147 us -> 0 us
  Pallas kernels: 0 us -> 86.2 us
  local copies, waits for them, and re-layouts: 40.1 us -> 3.27 us
  starting transfers between devices: 22.9 us -> 0 us
  between operations: 13.6 us -> 0.05 us
  matrix products: 7.83 us -> 0 us
  other arithmetic: 9.02 us -> 2.75 us
    all_gather x2 -> x0, waiting for transfers between devices: 102 us -> none  [local(): whole_acts = lax.all_gather(activity, 'neuron', axis=1, tiled=True)]
    pallas_call x0 -> x1, Pallas kernels: none -> 86.2 us  [local(): pl.pallas_call(functools.partial(kernel, layers, devices, own, capacity),...]
    all_to_all x4 -> x0, waiting for transfers between devices: 44.8 us -> none  [the longest x2 44.8 us: local(): lax.all_to_all(outgoing, 'neuron', split_axis=0, concat_axis=0, tiled=True)]
    scatter x4 -> x0, local copies, waits for them, and re-layouts: 29.3 us -> none  [the longest x2 27.4 us: local(): outgoing = jnp.zeros((devices * capacity, image_rows, block_width), jnp.f...]
    all_to_all x4 -> x0, starting transfers between devices: 22.9 us -> none  [the longest x2 14.2 us: local(): lax.all_to_all(labels, 'neuron', split_axis=0, concat_axis=0, tiled=True)]
    dot_general x4 -> x0, matrix products: 7.83 us -> none  [the longest x2 6.35 us: local(): jnp.einsum('bsk,skn->sbn', picked, tile_weights[layer_index], preferred_e...]
    reshape x2 -> x1, local copies, waits for them, and re-layouts: 3.9 us -> 0.09 us  [tables(): jnp.transpose(place.reshape(layers, devices, own), (1, 0, 2))]
    convert_element_type x4 -> x0, other arithmetic: 3.04 us -> none  [the longest x2 1.64 us: local(): jnp.clip(summed + bias[layer_index][None, :], 0.0, CEILING)]
  transfers between devices with their start and end apart: 6 -> 0, of which waited for: 4 -> 0; matrix products, arithmetic and copies ran while one was open for 22% -> 0% of each run, Pallas kernels for 0% -> 0%
where the time goes in v1:
time: 93.1 us; the launch traced here: 92.2 us
  Pallas kernels  86.2 us (93%)
  local copies, waits for them, and re-layouts  3.27 us (4%)
  other arithmetic  2.75 us (3%)
    pallas_call x1, Pallas kernels, local(): pl.pallas_call(functools.partial(kernel, layers, devices, own, capacity),...  86.2 us
    unnamed x5, local copies, waits for them, and re-layouts  2.31 us

profile of v1, /device:TPU:0, one launch (start us, length us, event | category | flops | bytes accessed | tf_op | source)
XLA Modules:
  0.0 92.2 jit_solution(15780336486742619929)
XLA Ops:
  0.0 0.8 fusion.3
  0.8 0.7 fusion
  1.5 0.7 fusion.2
  2.2 0.2 convert_reduce_fusion
  2.4 0.7 add_add_fusion
  3.1 0.1 select_reduce_fusion.2
  3.3 0.2 select_reduce_fusion
  3.5 0.1 add.50
  3.6 0.1 reshape.161
  3.7 0.0 copy-start
  3.7 0.9 copy-done
  4.6 0.0 copy-start.1
  4.6 0.8 copy-done.1
  5.4 86.2 %shard_map.55 = bf16[16,4096]{1,0:T(8,128)(2,1)S(1)} custom-call(s32[512]{0:T(512)S(1)} %bitcast.11, s32[16,1,128]{2,1,0:T(1,128)S(1)} %pad.4.place, bf16[16,4096]{1,0:T(8,128)(2,1)S(1)} %copy-done, bf16[2,128,128,128]{3,2,1,0:T(8,128)(2,1)} %weights_hbm.1, f32[2,4096]{1,0:T(2,128)S(1)} %copy-done.1), custom_call_target="tpu_custom_call" | custom-call | tf_op jit(solution)/shard_map/pallas_call | solution.py:298
  91.6 0.7 copy.12
  (6 shorter events, 0.1 us)
Async XLA Ops:
  3.7 0.9 copy-start
  4.6 0.8 copy-start.1

commit v2 on v1

--- a/solution.py
+++ b/solution.py
@@ -8,7 +8,8 @@
 from jax.sharding import PartitionSpec as P
 
 CEILING = 32.0
-SENT = (jnp.float32, jnp.bfloat16)
+NEAR, FAR = jnp.float32, jnp.bfloat16
+GROUP = 4
 
 
 def sides(devices):
@@ -32,8 +33,8 @@
 
 def kernel(
     layers, devices, own, capacity,
-    table, place, images, weights_hbm, bias, out,
-    acts, weights, outgoing, incoming, place_in, place_smem,
+    counts, blocks, images, weights_hbm, bias, out,
+    acts, weights, far_out, near_out, far_in, near_in, table_out, table, place, place_in, place_smem,
     weight_sem, place_send, place_recv, smem_sem,
     z_send, z_recv, half_send, half_recv, pass_send, part_send, part_recv,
 ):
@@ -54,13 +55,10 @@
         copy.start()
         return copy
 
+    far = devices // 2
+
     def partner(t):
-        q, i = t // (ys * xs), t % (ys * xs)
-        return index(
-            paired(z, zs - 1 - q, zs),
-            paired(y, ys - 1 - i // xs, ys),
-            paired(x, xs - 1 - i % xs, xs),
-        )
+        return paired(me, devices - 1 - t, devices)
 
     loads = []
     for layer in range(layers):
@@ -80,17 +78,52 @@
     for c in range(own):
         acts[0][me * own + c] = images[:, c * 128 : (c + 1) * 128]
     for layer in range(layers):
-        incoming[layer][slots] = jnp.zeros(incoming[layer].shape[1:], incoming[layer].dtype)
-    place_in[me] = place[me]
+        for buf in (far_in[layer], near_in[layer]):
+            buf[far * capacity] = jnp.zeros(buf.shape[1:], buf.dtype)
     pl.semaphore_wait(barrier, devices - 1)
+    chunk_at = lax.rem(me * own, 128)
 
     def place_copy(t):
         target = partner(t)
         return pltpu.make_async_remote_copy(
-            src_ref=place.at[target], dst_ref=place_in.at[me],
+            src_ref=place.at[(target * own) // 128], dst_ref=place_in.at[me],
             send_sem=place_send.at[t], recv_sem=place_recv.at[me],
             device_id={"neuron": target}, device_id_type=pl.DeviceIdType.MESH,
         )
+
+    def make_tables():
+        total = blocks.shape[1]
+        for layer in range(layers):
+            both = blocks[layer]
+            row_of, col_of = both[:, 0:1], both[:, 1:2]
+            slot_of = lax.broadcasted_iota(jnp.int32, (total, total), 0)
+            other = lax.broadcasted_iota(jnp.int32, (total, total), 1)
+            usable = slot_of[:, 0:1] < counts[layer, 0]
+            owner = jnp.where(usable, col_of // own, -1)
+            wide = jnp.broadcast_to(owner, (total, total)).astype(jnp.float32)
+            same = (wide == wide.T) & (other < slot_of)
+            rank = jnp.sum(jnp.where(same, 1.0, 0.0), axis=1, keepdims=True).astype(jnp.int32)
+            spot = jnp.where(usable, owner * capacity + rank, -1)
+            hit = spot == lax.broadcasted_iota(jnp.int32, (total, slots), 1)
+            table_out[2 * layer] = jnp.sum(jnp.where(hit, row_of, 0), axis=0, keepdims=True)
+            table_out[2 * layer + 1] = jnp.sum(
+                jnp.where(hit, slot_of[:, 0:1], 0), axis=0, keepdims=True
+            )
+            empty = far * capacity
+            column = jnp.where(usable, col_of, -1)
+            term = paired_term(owner) * capacity + rank - empty
+            for chunk in range(devices * own // 128):
+                lane = lax.broadcasted_iota(jnp.int32, (total, 128), 1) + chunk * 128
+                place[chunk, layer] = empty + jnp.sum(
+                    jnp.where(column == lane, term, 0), axis=0, keepdims=True
+                )
+
+    def paired_term(owner):
+        distance, bit = jnp.zeros_like(owner), 1
+        while bit < devices:
+            distance = distance + jnp.where((owner // bit) % 2 == (me // bit) % 2, 0, bit)
+            bit *= 2
+        return lax.rem(devices - 1 - distance, far)
 
     for layer in range(layers):
         pending = []
@@ -159,6 +192,12 @@
 
         spread(0)
         if layer == 0:
+            make_tables()
+            place_in[me] = place[(me * own) // 128]
+            to_table = pltpu.make_async_copy(table_out, table, smem_sem)
+            to_table.start()
+            to_table.wait()
+
             def send_place(t, carry):
                 place_copy(t).start()
                 return carry
@@ -184,33 +223,48 @@
                         arrived(piece(owner, part), half_recv.at[layer, owner, part])
         loads[layer].wait()
 
-        out_buf, in_buf = outgoing[layer], incoming[layer]
-
-        def product(target, k):
-            at = layer * 2 * slots + target * capacity + k
-            block = acts[layer][table[at]]
-            tile = weights[layer][table[at + slots]]
-            return jnp.dot(block, tile, preferred_element_type=jnp.float32).astype(out_buf.dtype)
-
-        def part_copy(t):
+        def product(target, k, kind):
+            at = target * capacity + k
+            block = acts[layer][table[2 * layer, 0, at]]
+            tile = weights[layer][table[2 * layer + 1, 0, at]]
+            return jnp.dot(block, tile, preferred_element_type=jnp.float32).astype(kind)
+
+        def buffers(is_far):
+            if is_far:
+                return far_out[layer], far_in[layer], 0
+            return near_out[layer], near_in[layer], far
+
+        def part_copy(t, is_far):
+            sent, got, base = buffers(is_far)
+            rows = pl.ds((t - base) * capacity, capacity)
+            return pltpu.make_async_remote_copy(
+                src_ref=sent.at[rows], dst_ref=got.at[rows],
+                send_sem=part_send.at[layer, t], recv_sem=part_recv.at[layer, t],
+                device_id={"neuron": partner(t)}, device_id_type=pl.DeviceIdType.MESH,
+            )
+
+        def fill(t, is_far, to):
             target = partner(t)
-            return pltpu.make_async_remote_copy(
-                src_ref=out_buf.at[pl.ds(target * capacity, capacity)],
-                dst_ref=in_buf.at[pl.ds(me * capacity, capacity)],
-                send_sem=part_send.at[layer, t], recv_sem=part_recv.at[layer, me],
-                device_id={"neuron": target}, device_id_type=pl.DeviceIdType.MESH,
-            )
-
-        def step(t, carry):
-            target = partner(t)
+            base = buffers(is_far)[2]
             for k in range(capacity):
-                out_buf[target * capacity + k] = product(target, k)
-            part_copy(t).start()
+                to[(t - base) * capacity + k] = product(target, k, to.dtype)
+
+        group = GROUP if far % GROUP == 0 else 1
+
+        def step(is_far, base, g, carry):
+            for i in range(group):
+                fill(base + g * group + i, is_far, buffers(is_far)[0])
+            for i in range(group):
+                part_copy(base + g * group + i, is_far).start()
             return carry
 
-        lax.fori_loop(0, devices - 1, step, 0)
-        for k in range(capacity):
-            in_buf[me * capacity + k] = product(me, k)
+        lax.fori_loop(0, far // group, functools.partial(step, True, 0), 0)
+        lax.fori_loop(0, far // group - 1, functools.partial(step, False, far), 0)
+        for t in range(devices - group, devices - 1):
+            fill(t, False, near_out[layer])
+        for t in range(devices - group, devices - 1):
+            part_copy(t, False).start()
+        fill(devices - 1, False, near_in[layer])
 
         if layer == 0:
             def take_place(t, carry):
@@ -223,21 +277,21 @@
             to_smem.start()
             to_smem.wait()
 
-        def take_part(t, carry):
-            source = partner(t)
-            ref = in_buf.at[pl.ds(source * capacity, capacity)]
-            pltpu.make_async_copy(ref, ref, part_recv.at[layer, source]).wait()
+        def take_part(is_far, t, carry):
+            part_copy(t, is_far).wait_recv()
             return carry
 
-        lax.fori_loop(0, devices - 1, take_part, 0)
+        lax.fori_loop(far, devices - 1, functools.partial(take_part, False), 0)
+        lax.fori_loop(0, far, functools.partial(take_part, True), 0)
 
         def combine(c, carry):
             total = jnp.broadcast_to(
-                bias[pl.ds(layer, 1), pl.ds(pl.multiple_of(c * 128, 128), 128)], in_buf.shape[1:]
+                bias[pl.ds(layer, 1), pl.ds(pl.multiple_of(c * 128, 128), 128)],
+                near_in[layer].shape[1:],
             )
-            for source in range(devices):
-                at = place_smem[source, 0, layer * own + c]
-                total = total + in_buf[at].astype(jnp.float32)
+            for t in range(devices):
+                at = place_smem[partner(t), layer, 0, chunk_at + c]
+                total = total + buffers(t < far)[1][at].astype(jnp.float32)
             value = jnp.minimum(jnp.maximum(total, 0.0), CEILING).astype(jnp.bfloat16)
             if layer + 1 < layers:
                 acts[layer + 1][me * own + c] = value
@@ -250,36 +304,14 @@
         for copy in pending:
             copy.wait_send()
 
-        def drain(t, carry):
-            part_copy(t).wait_send()
+        def drain(is_far, t, carry):
+            part_copy(t, is_far).wait_send()
             if layer == 0:
                 place_copy(t).wait_send()
             return carry
 
-        lax.fori_loop(0, devices - 1, drain, 0)
-
-
-def tables(tile_blocks, tile_count, devices, own, capacity):
-    layers, slot_total, _ = tile_blocks.shape
-    me = lax.axis_index("neuron")
-    slots = devices * capacity
-    row_ids, col_ids = tile_blocks[:, :, 0], tile_blocks[:, :, 1]
-    slot_ids = jnp.arange(slot_total, dtype=jnp.int32)
-    usable = slot_ids[None, :] < tile_count
-    owners = jnp.where(usable, col_ids // own, -1)
-    earlier = (owners[:, :, None] == owners[:, None, :]) & (slot_ids[None, :] < slot_ids[:, None])
-    rank = jnp.sum(earlier.astype(jnp.int32), axis=2)
-    dest = jnp.where(usable, owners * capacity + rank, -1)
-    hit = dest[:, None, :] == jnp.arange(slots, dtype=jnp.int32)[:, None]
-    rows = jnp.sum(jnp.where(hit, row_ids[:, None, :], 0), axis=2)
-    tiles = jnp.sum(jnp.where(hit, slot_ids, 0), axis=2)
-    table = jnp.stack([rows, tiles], axis=1).reshape(-1)
-    live_cols = jnp.where(usable, col_ids, -1)
-    match = live_cols[:, None, :] == jnp.arange(devices * own, dtype=jnp.int32)[:, None]
-    place = slots + jnp.sum(jnp.where(match, me * capacity + rank[:, None, :] - slots, 0), axis=2)
-    place = jnp.transpose(place.reshape(layers, devices, own), (1, 0, 2)).reshape(devices, 1, layers * own)
-    width = -(-layers * own // 128) * 128
-    return table, jnp.pad(place, ((0, 0), (0, 0), (0, width - layers * own)))
+        lax.fori_loop(0, far, functools.partial(drain, True), 0)
+        lax.fori_loop(far, devices - 1, functools.partial(drain, False), 0)
 
 
 def local(images, tile_weights, tile_blocks, tile_count, bias):
@@ -290,9 +322,8 @@
     capacity = max(2, slot_total // devices)
     slots = devices * capacity
     zs, ys, xs = sides(devices)
-    table, place = tables(tile_blocks, tile_count, devices, own, capacity)
-    width = place.shape[2]
-    sent = [SENT[min(layer, len(SENT) - 1)] for layer in range(layers)]
+    half_slots = slots // 2
+    chunks = devices * own // 128
     fan = 2 * (ys + xs)
     vmem = pl.BlockSpec(memory_space=pltpu.VMEM)
     return pl.pallas_call(
@@ -306,10 +337,15 @@
         scratch_shapes=[
             [pltpu.VMEM((devices * own, image_rows, block), jnp.bfloat16)] * layers,
             [pltpu.VMEM((slot_total, block, block), jnp.bfloat16)] * layers,
-            [pltpu.VMEM((slots, image_rows, block), kind) for kind in sent],
-            [pltpu.VMEM((slots + 1, image_rows, block), kind) for kind in sent],
-            pltpu.VMEM((devices, 1, width), jnp.int32),
-            pltpu.SMEM((devices, 1, width), jnp.int32),
+            [pltpu.VMEM((half_slots, image_rows, block), FAR)] * layers,
+            [pltpu.VMEM((half_slots, image_rows, block), NEAR)] * layers,
+            [pltpu.VMEM((half_slots + 1, image_rows, block), FAR)] * layers,
+            [pltpu.VMEM((half_slots + 1, image_rows, block), NEAR)] * layers,
+            pltpu.VMEM((2 * layers, 1, slots), jnp.int32),
+            pltpu.SMEM((2 * layers, 1, slots), jnp.int32),
+            pltpu.VMEM((chunks, layers, 1, 128), jnp.int32),
+            pltpu.VMEM((devices, layers, 1, 128), jnp.int32),
+            pltpu.SMEM((devices, layers, 1, 128), jnp.int32),
             pltpu.SemaphoreType.DMA((layers,)),
             pltpu.SemaphoreType.DMA((devices,)),
             pltpu.SemaphoreType.DMA((devices,)),
@@ -325,7 +361,7 @@
         compiler_params=pltpu.CompilerParams(
             collective_id=0, has_side_effects=True, vmem_limit_bytes=48 * 1024 * 1024
         ),
-    )(table, place, images, tile_weights, bias)
+    )(tile_count, tile_blocks, images, tile_weights, bias)
 
 
 def solution(mesh):

time: 93.1 us -> 83.9 us (0.901)
  Pallas kernels: 86.2 us -> 79.5 us
  other arithmetic: 2.75 us -> 0 us
    pallas_call x1, Pallas kernels: 86.2 us -> 79.5 us  [local(): pl.pallas_call(functools.partial(kernel, layers, devices, own, capacity),...]
    unnamed x5 -> x7, local copies, waits for them, and re-layouts: 2.31 us -> 3.87 us
where the time goes in v2:
time: 83.9 us; the launch traced here: 83.4 us
  Pallas kernels  79.5 us (95%)
  local copies, waits for them, and re-layouts  3.87 us (5%)
    pallas_call x1, Pallas kernels, local(): pl.pallas_call(functools.partial(kernel, layers, devices, own, capacity),...  79.5 us
    unnamed x7, local copies, waits for them, and re-layouts  3.87 us

profile of v2, /device:TPU:0, one launch (start us, length us, event | category | flops | bytes accessed | tf_op | source)
XLA Modules:
  0.0 83.4 jit_solution(13848283766003033840)
XLA Ops:
  0.0 0.7 copy.6.counts
  0.7 0.8 copy.7.blocks
  1.6 0.0 copy-start
  1.6 0.9 %copy-done = bf16[16,4096]{1,0:T(8,128)(2,1)S(1)} copy-done((bf16[16,4096]{1,0:T(8,128)(2,1)S(1)}, bf16[16,4096]{1,0:T(8,128)(2,1)}, u32[]{:S(2)}) %copy-start) | copy-done | bytes 131096
  2.5 0.0 copy-start.1
  2.5 0.8 copy-done.1
  3.2 79.5 %shard_map.55 = bf16[16,4096]{1,0:T(8,128)(2,1)S(1)} custom-call(s32[2,1]{1,0:T(2,128)S(1)} %copy.6.counts, s32[2,128,2]{2,1,0:T(8,128)S(1)} %copy.7.blocks, bf16[16,4096]{1,0:T(8,128)(2,1)S(1)} %copy-done, bf16[2,128,128,128]{3,2,1,0:T(8,128)(2,1)} %weights_hbm.1, f32[2,4096]{1,0:T(2,128)S(1)} %copy-done.1), custom_call_target="tpu_custom_call" | custom-call | tf_op jit(solution)/shard_map/pallas_call | solution.py:329
  82.7 0.7 copy.9
Async XLA Ops:
  1.6 0.9 %copy-start = (bf16[16,4096]{1,0:T(8,128)(2,1)S(1)}, bf16[16,4096]{1,0:T(8,128)(2,1)}, u32[]{:S(2)}) copy-start(bf16[16,4096]{1,0:T(8,128)(2,1)} %images.1) | copy-start | bytes 393220
  2.5 0.8 copy-start.1

commit v3 on v2

--- a/solution.py
+++ b/solution.py
@@ -33,16 +33,18 @@
 
 def kernel(
     layers, devices, own, capacity,
-    counts, blocks, images, weights_hbm, bias, out,
+    counts, blocks, images_hbm, weights_hbm, bias_hbm, out,
     acts, weights, far_out, near_out, far_in, near_in, table_out, table, place, place_in, place_smem,
-    weight_sem, place_send, place_recv, smem_sem,
-    z_send, z_recv, half_send, half_recv, pass_send, part_send, part_recv,
+    images, bias, sums, early_sem, weight_sem, place_send, place_recv, smem_sem,
+    z_send, z_recv, half_send, half_recv, pass_send, part_send, part_recv, side_send, side_pass, side_recv,
 ):
     me = lax.axis_index("neuron")
     zs, ys, xs = sides(devices)
     z, y, x = me // (ys * xs), (me // xs) % ys, me % xs
     slots = devices * capacity
-    half = own // 2
+    side = own // 8
+    main = own - side
+    half = main // 2
 
     def index(zz, yy, xx):
         return (zz * ys + yy) * xs + xx
@@ -60,6 +62,12 @@
     def partner(t):
         return paired(me, devices - 1 - t, devices)
 
+    early = [
+        pltpu.make_async_copy(images_hbm, images, early_sem.at[0]),
+        pltpu.make_async_copy(bias_hbm, bias, early_sem.at[1]),
+    ]
+    for load in early:
+        load.start()
     loads = []
     for layer in range(layers):
         load = pltpu.make_async_copy(weights_hbm.at[layer], weights[layer], weight_sem.at[layer])
@@ -75,6 +83,7 @@
         return carry
 
     lax.fori_loop(0, devices - 1, greet, 0)
+    early[0].wait()
     for c in range(own):
         acts[0][me * own + c] = images[:, c * 128 : (c + 1) * 128]
     for layer in range(layers):
@@ -92,13 +101,16 @@
         )
 
     def make_tables():
-        total = blocks.shape[1]
+        total = blocks.shape[2]
         for layer in range(layers):
-            both = blocks[layer]
-            row_of, col_of = both[:, 0:1], both[:, 1:2]
+            row_of, col_of = (
+                jnp.broadcast_to(blocks[layer, i : i + 1, :], (total, total))
+                .astype(jnp.float32).T.astype(jnp.int32)[:, 0:1]
+                for i in range(2)
+            )
             slot_of = lax.broadcasted_iota(jnp.int32, (total, total), 0)
             other = lax.broadcasted_iota(jnp.int32, (total, total), 1)
-            usable = slot_of[:, 0:1] < counts[layer, 0]
+            usable = slot_of[:, 0:1] < counts[layer]
             owner = jnp.where(usable, col_of // own, -1)
             wide = jnp.broadcast_to(owner, (total, total)).astype(jnp.float32)
             same = (wide == wide.T) & (other < slot_of)
@@ -134,7 +146,29 @@
         def arrived(ref, sem):
             pltpu.make_async_copy(ref, ref, sem).wait()
 
-        mine = acts[layer].at[pl.ds(me * own, own)]
+        def side_of(owner):
+            return acts[layer].at[pl.ds(owner * own + main, side)]
+
+        def side_along_z(owner, row):
+            for m in range(1, zs):
+                pending.append(
+                    remote(side_of(owner), side_of(owner), side_pass.at[layer, row, m],
+                           side_recv.at[layer, owner], index(paired(z, m, zs), y, x))
+                )
+
+        mates = [(n, k) for n in range(ys) for k in range(xs) if n or k]
+
+        def mate(zz, row):
+            return index(zz, paired(y, mates[row][0], ys), paired(x, mates[row][1], xs))
+
+        if side:
+            for row in range(len(mates)):
+                pending.append(
+                    remote(side_of(me), side_of(me), side_send.at[layer, row],
+                           side_recv.at[layer, me], mate(z, row))
+                )
+
+        mine = acts[layer].at[pl.ds(me * own, main)]
         for m in range(1, zs):
             pending.append(
                 remote(mine, mine, z_send.at[layer, m], z_recv.at[layer, z],
@@ -145,7 +179,7 @@
             zz = paired(z, m, zs)
             owner = index(zz, y, x)
             if m:
-                shard = acts[layer].at[pl.ds(owner * own, own)]
+                shard = acts[layer].at[pl.ds(owner * own, main)]
                 arrived(shard, z_recv.at[layer, zz])
             slot = 0
             for first in (True, False):
@@ -191,6 +225,12 @@
                     slot += 1
 
         spread(0)
+        if side:
+            side_along_z(me, len(mates))
+            for row in range(len(mates)):
+                owner = mate(z, row)
+                arrived(side_of(owner), side_recv.at[layer, owner])
+                side_along_z(owner, row)
         if layer == 0:
             make_tables()
             place_in[me] = place[(me * own) // 128]
@@ -207,6 +247,12 @@
             spread(m)
             relay(m - 1)
         relay(zs - 1)
+
+        if side:
+            for m in range(1, zs):
+                zz = paired(z, m, zs)
+                for owner in [index(zz, y, x)] + [mate(zz, row) for row in range(len(mates))]:
+                    arrived(side_of(owner), side_recv.at[layer, owner])
 
         for m in range(zs):
             zz = paired(z, m, zs)
@@ -281,17 +327,28 @@
             part_copy(t, is_far).wait_recv()
             return carry
 
-        lax.fori_loop(far, devices - 1, functools.partial(take_part, False), 0)
-        lax.fori_loop(0, far, functools.partial(take_part, True), 0)
-
-        def combine(c, carry):
-            total = jnp.broadcast_to(
+        def terms(c, total, first):
+            for t in range(first, first + far):
+                at = place_smem[partner(t), layer, 0, chunk_at + c]
+                total = total + buffers(t < far)[1][at].astype(jnp.float32)
+            return total
+
+        def combine_near(c, carry):
+            start = jnp.broadcast_to(
                 bias[pl.ds(layer, 1), pl.ds(pl.multiple_of(c * 128, 128), 128)],
                 near_in[layer].shape[1:],
             )
-            for t in range(devices):
-                at = place_smem[partner(t), layer, 0, chunk_at + c]
-                total = total + buffers(t < far)[1][at].astype(jnp.float32)
+            sums[c] = terms(c, start, far)
+            return carry
+
+        if layer == 0:
+            early[1].wait()
+        lax.fori_loop(far, devices - 1, functools.partial(take_part, False), 0)
+        lax.fori_loop(0, own, combine_near, 0)
+        lax.fori_loop(0, far, functools.partial(take_part, True), 0)
+
+        def combine(c, carry):
+            total = terms(c, sums[c], 0)
             value = jnp.minimum(jnp.maximum(total, 0.0), CEILING).astype(jnp.bfloat16)
             if layer + 1 < layers:
                 acts[layer + 1][me * own + c] = value
@@ -326,12 +383,12 @@
     chunks = devices * own // 128
     fan = 2 * (ys + xs)
     vmem = pl.BlockSpec(memory_space=pltpu.VMEM)
+    hbm = pl.BlockSpec(memory_space=pltpu.HBM)
     return pl.pallas_call(
         functools.partial(kernel, layers, devices, own, capacity),
         out_shape=jax.ShapeDtypeStruct((image_rows, local_width), jnp.bfloat16),
         in_specs=[
-            pl.BlockSpec(memory_space=pltpu.SMEM), vmem, vmem,
-            pl.BlockSpec(memory_space=pl.ANY), vmem,
+            pl.BlockSpec(memory_space=pltpu.SMEM), vmem, hbm, hbm, hbm,
         ],
         out_specs=vmem,
         scratch_shapes=[
@@ -346,6 +403,10 @@
             pltpu.VMEM((chunks, layers, 1, 128), jnp.int32),
             pltpu.VMEM((devices, layers, 1, 128), jnp.int32),
             pltpu.SMEM((devices, layers, 1, 128), jnp.int32),
+            pltpu.VMEM((image_rows, local_width), jnp.bfloat16),
+            pltpu.VMEM((layers, local_width), jnp.float32),
+            pltpu.VMEM((own, image_rows, block), jnp.float32),
+            pltpu.SemaphoreType.DMA((2,)),
             pltpu.SemaphoreType.DMA((layers,)),
             pltpu.SemaphoreType.DMA((devices,)),
             pltpu.SemaphoreType.DMA((devices,)),
@@ -357,11 +418,14 @@
             pltpu.SemaphoreType.DMA((layers, zs, 2 * ys * xs)),
             pltpu.SemaphoreType.DMA((layers, devices)),
             pltpu.SemaphoreType.DMA((layers, devices)),
+            pltpu.SemaphoreType.DMA((layers, ys * xs)),
+            pltpu.SemaphoreType.DMA((layers, ys * xs, zs)),
+            pltpu.SemaphoreType.DMA((layers, devices)),
         ],
         compiler_params=pltpu.CompilerParams(
-            collective_id=0, has_side_effects=True, vmem_limit_bytes=48 * 1024 * 1024
+            collective_id=0, has_side_effects=True, vmem_limit_bytes=67043328
         ),
-    )(tile_count, tile_blocks, images, tile_weights, bias)
+    )(tile_count.reshape(-1), jnp.transpose(tile_blocks, (0, 2, 1)), images, tile_weights, bias)
 
 
 def solution(mesh):

time: 83.9 us -> 82.5 us (0.983)
  local copies, waits for them, and re-layouts: 3.87 us -> 1.57 us
  Pallas kernels: 79.5 us -> 80.7 us
    unnamed x7 -> x1, local copies, waits for them, and re-layouts: 3.87 us -> 1.57 us
    pallas_call x1, Pallas kernels: 79.5 us -> 80.7 us  [local(): pl.pallas_call(functools.partial(kernel, layers, devices, own, capacity),...]
where the time goes in v3:
time: 82.5 us; the launch traced here: 82.3 us
  Pallas kernels  80.7 us (98%)
  local copies, waits for them, and re-layouts  1.57 us (2%)
    pallas_call x1, Pallas kernels, local(): pl.pallas_call(functools.partial(kernel, layers, devices, own, capacity),...  80.7 us

profile of v3, /device:TPU:0, one launch (start us, length us, event | category | flops | bytes accessed | tf_op | source)
XLA Modules:
  0.0 82.3 jit_solution(5949101258742836160)
XLA Ops:
  0.0 80.7 %shard_map.55 = bf16[16,4096]{1,0:T(8,128)(2,1)} custom-call(s32[2]{0:T(128)} %bitcast.3, s32[2,2,128]{2,1,0:T(2,128)} %bitcast.2, bf16[16,4096]{1,0:T(8,128)(2,1)} %images_hbm.1, bf16[2,128,128,128]{3,2,1,0:T(8,128)(2,1)} %weights_hbm.1, f32[2,4096]{1,0:T(2,128)} %bias_hbm.1), custom_call_target="tpu_custom_call" | custom-call | tf_op jit(solution)/shard_map/pallas_call | solution.py:387
  80.7 1.6 %copy.7 = bf16[16,4096]{1,0:T(8,128)(2,1)} copy(bf16[16,4096]{1,0:T(8,128)(2,1)} %shard_map.55) | data formatting | bytes 262144
